TPU v7x, 128 devices: a whole 4x4x4 slice. The times are simulated.
128 devices in a mesh: dp: 4 (over x), fsdp: 8 (over y, core), enc: 4 (over z).
Axes of the slice: x: 4, y: 4, z: 4, core: 2. Of those that a mesh axis runs over, the one named last changes fastest.
Arguments:
- hidden: bfloat16 [32768, 8192], P(('dp', 'fsdp', 'enc')), may hold values from -40 to 40
- residual_gradient: bfloat16 [32768, 8192], P(('dp', 'fsdp', 'enc')), may hold values from -3 to 3
- value_output_gradient: bfloat16 [32768, 1024], P(('dp', 'fsdp', 'enc')), may hold values from -6 to 6
- attention_norm_gain: float32 [8192], replicated, may hold values from 0.1 to 1.9
- value_frozen_weight: bfloat16 [8192, 1024], P('fsdp'), may hold values from -0.0625 to 0.0625
- value_down_factor: bfloat16 [8192, 16], replicated, may hold values from -0.0625 to 0.0625
- value_up_factor: bfloat16 [16, 1024], replicated, may hold values from -0.29882812 to 0.29882812
- merger_frozen_weight: bfloat16 [5120, 8192], P(None, ('fsdp', 'enc')), may hold values from -0.078125 to 0.078125
- merger_down_factor: bfloat16 [5120, 16], replicated, may hold values from -0.078125 to 0.078125
- merger_up_factor: bfloat16 [16, 8192], P(None, ('fsdp', 'enc')), may hold values from -0.29882812 to 0.29882812
- merger_saved_preactivation: bfloat16 [4096, 5120], P(('dp', 'fsdp', 'enc')), may hold values from -5 to 5
- image_token_counts: int32 [128], P('dp'), may hold values from 8 to 16, as said below
- image_encoder_owner: int32 [128], P('dp'), may hold values from 0 to 31, as said below
- image_first_rows: int32 [128], P(('dp', 'fsdp', 'enc')), may hold values from 0 to 255, as said below
Outputs:
- layer_input_gradient: bfloat16 [32768, 8192], P(('dp', 'fsdp', 'enc'))
- preactivation_gradient: bfloat16 [4096, 5120], P(('dp', 'fsdp', 'enc'))
- value_down_gradient: float32 [8192, 16], replicated
- value_up_gradient: float32 [16, 1024], replicated
- merger_down_gradient: float32 [5120, 16], replicated
- merger_up_gradient: float32 [16, 8192], P(None, ('fsdp', 'enc'))
Inputs may be any that keep to these rules, and one draw needn't show every extreme that they name: `image_token_counts`: within each data replica some encoder device owns exactly 2 images, all of 16 visual tokens, so its rows fill all 32; no other device owns more than 2 images. `image_encoder_owner`: encoder devices are numbered within the data replica in mesh order. `image_first_rows`: images of one device lie inside its 256 rows in increasing order and don't intersect.
All inputs are finite; a program needn't handle non-finite values.
Results may differ from a plain program's by a relative error of at most 0.0085.
Values may be sent and summed in bfloat16 or wider, within the bound.
A program may use at most 192 MiB of HBM per device.

v0:
```python
import jax
import jax.numpy as jnp
from jax import lax
from jax.sharding import PartitionSpec as P

MAXIMG = 16
adapter_scale = 2.0
norm_eps = 1e-06


def laid_out(blocks, dim):
    shape = list(blocks.shape[1:])
    shape[dim] *= blocks.shape[0]
    return jnp.moveaxis(blocks, 0, dim).reshape(shape)


def sent_to_all(value, axis):
    copies = jnp.broadcast_to(value, (lax.axis_size(axis), *value.shape))
    return lax.all_to_all(copies, axis, split_axis=0, concat_axis=0, tiled=True)


def gathered_copies(value, axis, dim):
    return laid_out(sent_to_all(value, axis), dim)


def in_one_piece(arrays, axis, dim, along):
    widths = [a.shape[along] for a in arrays]
    both = jnp.concatenate(arrays, axis=along)
    out = lax.psum_scatter(both, axis, scatter_dimension=dim, tiled=True)
    return tuple(jnp.split(out, [sum(widths[:k]) for k in range(1, len(widths))], axis=along))


def over_copies(value, axis):
    return sent_to_all(value, axis).sum(axis=0)


def gelu_parts(preact):
    normal_cdf = 0.5 * (1.0 + lax.erf(preact * 0.7071067811865476))
    normal_pdf = jnp.exp(-0.5 * preact * preact) * 0.3989422804014327
    return (normal_cdf, normal_pdf)


def owner_layout(image_token_counts, image_encoder_owner, owner_count, owner_room, slot_len):
    total_images = image_token_counts.shape[0]
    image_ids = jnp.arange(total_images)
    same_owner = image_encoder_owner[:, None] == image_encoder_owner[None, :]
    earlier = image_ids[None, :] < image_ids[:, None]
    starts = jnp.sum(jnp.where(same_owner & earlier, image_token_counts[None, :], 0), axis=1)
    row_index = jnp.arange(owner_count * owner_room)
    row_owner = row_index // owner_room
    row_place = row_index % owner_room
    matches = (
        (row_owner[:, None] == image_encoder_owner[None, :])
        & (row_place[:, None] >= starts[None, :])
        & (row_place[:, None] < (starts + image_token_counts)[None, :])
    )
    source = jnp.sum(
        jnp.where(matches, image_ids[None, :] * slot_len + row_place[:, None] - starts[None, :], 0),
        axis=1,
    )
    valid_rows = jnp.any(matches, axis=1)
    return (source, valid_rows)


def take_slots(layer_input_gradient, counts_in, offsets_in):
    padded = jnp.concatenate(
        [
            layer_input_gradient,
            jnp.zeros((MAXIMG, layer_input_gradient.shape[1]), layer_input_gradient.dtype),
        ],
        axis=0,
    )
    window = lax.dynamic_slice_in_dim(padded, offsets_in[0], MAXIMG, 0)
    inside = jnp.arange(MAXIMG) < counts_in[0]
    pieces = jnp.where(inside[:, None], window, jnp.zeros_like(window))
    return pieces


def decoder_layer_block(
    incoming_rows,
    residual_input,
    value_incoming,
    attention_norm_gain,
    passed_gradient,
    value_down_factor,
    value_up_factor,
):
    values = incoming_rows.astype(jnp.float32)
    inverse = lax.rsqrt(jnp.mean(values * values, axis=1, keepdims=True) + norm_eps)
    normalized_input = (values * inverse * attention_norm_gain).astype(jnp.bfloat16)
    value_low_product = jnp.dot(
        value_incoming, value_up_factor.T, preferred_element_type=jnp.float32
    ).astype(jnp.bfloat16)
    normalized_gradient = passed_gradient.astype(jnp.float32) + adapter_scale * jnp.dot(
        value_low_product, value_down_factor.T, preferred_element_type=jnp.float32
    )
    gained = attention_norm_gain * normalized_gradient
    layer_input_gradient = (
        residual_input.astype(jnp.float32)
        + inverse * gained
        - values * inverse**3 * jnp.mean(values * gained, axis=1, keepdims=True)
    ).astype(jnp.bfloat16)
    projected_rows = jnp.dot(
        normalized_input, value_down_factor, preferred_element_type=jnp.float32
    ).astype(jnp.bfloat16)
    up_term = lax.dot_general(
        projected_rows, value_incoming, (((0,), (0,)), ((), ())), preferred_element_type=jnp.float32
    )
    down_term = lax.dot_general(
        normalized_input,
        value_low_product,
        (((0,), (0,)), ((), ())),
        preferred_element_type=jnp.float32,
    )
    return (layer_input_gradient, down_term, up_term)


def body(
    hidden,
    residual_gradient,
    value_output_gradient,
    attention_norm_gain,
    value_frozen_weight,
    value_down_factor,
    value_up_factor,
    merger_frozen_weight,
    merger_down_factor,
    merger_up_factor,
    merger_saved_preactivation,
    image_token_counts,
    image_encoder_owner,
    image_first_rows,
):
    device_total = lax.axis_size("dp") * lax.axis_size("fsdp") * lax.axis_size("enc")
    gradient_scale = 256.0 / (hidden.shape[0] * device_total)
    scale_factor = gradient_scale * adapter_scale
    owner_count = lax.axis_size("fsdp") * lax.axis_size("enc")
    owner_room = merger_saved_preactivation.shape[0]
    preact = merger_saved_preactivation.astype(jnp.float32)
    normal_cdf, normal_pdf = gelu_parts(preact)
    activation = (preact * normal_cdf).astype(jnp.bfloat16)
    act_low = jnp.dot(activation, merger_down_factor, preferred_element_type=jnp.float32).astype(
        jnp.bfloat16
    )
    all_low = gathered_copies(act_low, ("fsdp", "enc"), 0)
    columns = lax.dot_general(
        lax.all_gather(value_output_gradient, "fsdp", axis=0, tiled=True),
        value_frozen_weight,
        (((1,), (1,)), ((), ())),
        preferred_element_type=jnp.float32,
    ).astype(jnp.bfloat16)
    passed_gradient = lax.all_to_all(columns, "fsdp", split_axis=0, concat_axis=1, tiled=True)
    layer_input_gradient, down_term, up_term = decoder_layer_block(
        hidden,
        residual_gradient,
        value_output_gradient,
        attention_norm_gain,
        passed_gradient,
        value_down_factor,
        value_up_factor,
    )
    member = lax.axis_index(("fsdp", "enc"))
    local_images = image_first_rows.shape[0]
    local_counts = lax.dynamic_slice_in_dim(
        image_token_counts, member * local_images, local_images, 0
    )
    slots_out = take_slots(layer_input_gradient, local_counts, image_first_rows)
    received = lax.all_to_all(slots_out, ("fsdp", "enc"), split_axis=1, concat_axis=0, tiled=True)
    source, valid_rows = owner_layout(
        image_token_counts, image_encoder_owner, owner_count, owner_room, MAXIMG
    )
    visual_tokens = jnp.where(
        valid_rows[:, None], jnp.take(received, source, axis=0), jnp.zeros((), received.dtype)
    )
    value_partial_sum = lax.dot_general(
        visual_tokens,
        merger_frozen_weight,
        (((1,), (1,)), ((), ())),
        preferred_element_type=jnp.float32,
    )
    low_part = lax.dot_general(
        visual_tokens,
        merger_up_factor,
        (((1,), (1,)), ((), ())),
        preferred_element_type=jnp.float32,
    )
    value_partial_sum = value_partial_sum + adapter_scale * jnp.dot(
        low_part, merger_down_factor.astype(jnp.float32).T
    )
    combined_gradient, low_sum = in_one_piece((value_partial_sum, low_part), ("fsdp", "enc"), 0, 1)
    preactivation_gradient = (combined_gradient * (normal_cdf + preact * normal_pdf)).astype(
        jnp.bfloat16
    )
    term_a2 = lax.dot_general(
        activation,
        low_sum.astype(jnp.bfloat16),
        (((0,), (0,)), ((), ())),
        preferred_element_type=jnp.float32,
    )
    term_b2 = lax.dot_general(
        all_low, visual_tokens, (((0,), (0,)), ((), ())), preferred_element_type=jnp.float32
    )
    merger_up_gradient = over_copies(scale_factor * term_b2, "dp")
    value_down_gradient, value_up_gradient, merger_down_gradient = lax.psum(
        (scale_factor * down_term, scale_factor * up_term, scale_factor * term_a2),
        ("dp", "fsdp", "enc"),
    )
    return (
        layer_input_gradient,
        preactivation_gradient,
        value_down_gradient,
        value_up_gradient,
        merger_down_gradient,
        merger_up_gradient,
    )


def solution(mesh):
    placed = (
        P(("dp", "fsdp", "enc"), None),
        P(("dp", "fsdp", "enc"), None),
        P(("dp", "fsdp", "enc"), None),
        P(),
        P("fsdp", None),
        P(),
        P(),
        P(None, ("fsdp", "enc")),
        P(),
        P(None, ("fsdp", "enc")),
        P(("dp", "fsdp", "enc"), None),
        P("dp"),
        P("dp"),
        P(("dp", "fsdp", "enc")),
    )
    return jax.shard_map(
        body,
        mesh=mesh,
        in_specs=placed,
        out_specs=(
            P(("dp", "fsdp", "enc"), None),
            P(("dp", "fsdp", "enc"), None),
            P(),
            P(),
            P(),
            P(None, ("fsdp", "enc")),
        ),
        check_vma=False,
    )
```

profile of v0, /device:TPU:1, one launch (start us, length us, event | category | flops | bytes accessed | tf_op | source)
XLA Modules:
  0.0 477.0 jit_solution(13086993412335632943)
XLA Ops:
  7.2 0.7 all-gather.2.cloned.1.call-update
  7.9 37.5 %all-gather.2.cloned.1.call-done = bf16[2048,1024]{1,0:T(8,128)(2,1)} async-done(((bf16[256,1024]{1,0:T(8,128)(2,1)}), bf16[2048,1024]{1,0:T(8,128)(2,1)}) %all-gather.2.cloned.1.call-update) | async-done | bytes 4194320 | tf_op jit(solution)/shard_map/all_gather | solution.py:147
  45.4 9.4 %convolution_convert_fusion = bf16[2048,1024]{1,0:T(8,128)(2,1)} fusion(bf16[2048,1024]{1,0:T(8,128)(2,1)} %all-gather.2.cloned.1.call-done, bf16[1024,1024]{1,0:T(8,128)(2,1)} %param.18), kind=kOutput, calls=%fused_computation.21 | convolution fusion | flops 4297064448 | bytes 10485760 | tf_op jit(solution)/shard_map/dot_general | solution.py:146
  54.9 4.9 %all-to-all-start = ((bf16[8,256,1024]{2,1,0:T(8,128)(2,1)}), bf16[8,256,1024]{2,1,0:T(8,128)(2,1)}, u32[]{:S(2)}, u32[]{:S(2)}) async-start(bf16[8,256,1024]{2,1,0:T(8,128)(2,1)} %bitcast.44), calls=%async_computation | async-start | bytes 8388608 | tf_op jit(solution)/shard_map/all_to_all | solution.py:152
  61.2 0.7 iota_compare_fusion.1
  62.2 46.3 %all-to-all-done = bf16[8,256,1024]{2,1,0:T(8,128)(2,1)} async-done(((bf16[8,256,1024]{2,1,0:T(8,128)(2,1)}), bf16[8,256,1024]{2,1,0:T(8,128)(2,1)}, u32[]{:S(2)}, u32[]{:S(2)}) %all-to-all-start) | async-done | bytes 4194336 | tf_op jit(solution)/shard_map/all_to_all | solution.py:152
  108.5 3.2 convert_bitcast_fusion
  111.8 1.7 copy.40
  113.4 4.9 %fusion.2 = (f32[256]{0:T(256)S(1)}, f32[256]{0:T(256)S(1)}, f32[256,8192]{1,0:T(8,128)S(1)}) fusion(bf16[256,8192]{1,0:T(8,128)(2,1)} %param.14, f32[256,8192]{1,0:T(8,128)S(1)} %bitcast.43, bf16[256,16]{0,1:T(8,128)(2,1)S(1)} %convolution_convert_fusion.1, bf16[8192,16]{0,1:T(8,128)(2,1)} %param.19, f32[8192]{0:T(1024)S(1)} %copy-done.8), kind=kOutput, calls=%fused_computation.11 | convolution fusion | flops 83885568 | bytes 21276672 | tf_op jit(solution)/shard_map/dot_general | solution.py:94
  118.4 3.4 fusion.5
  121.8 2.0 copy-done.3
  124.0 0.7 copy.42
  124.7 6.1 %all-to-all-start.1 = ((bf16[16,32,256]{2,0,1:T(8,128)(2,1)}), bf16[16,32,256]{2,0,1:T(8,128)(2,1)S(1)}, u32[]{:S(2)}, u32[]{:S(2)}) async-start(bf16[16,32,256]{2,0,1:T(8,128)(2,1)} %bitcast.38), calls=%async_computation.1 | async-start | bytes 524288 | tf_op jit(solution)/shard_map/all_to_all | solution.py:168
  131.2 8.4 %all-to-all-done.1 = bf16[16,32,256]{2,0,1:T(8,128)(2,1)S(1)} async-done(((bf16[16,32,256]{2,0,1:T(8,128)(2,1)}), bf16[16,32,256]{2,0,1:T(8,128)(2,1)S(1)}, u32[]{:S(2)}, u32[]{:S(2)}) %all-to-all-start.1) | async-done | bytes 262176 | tf_op jit(solution)/shard_map/all_to_all | solution.py:168
  139.6 5.0 %gather_fusion = bf16[1024,256]{1,0:T(8,128)(2,1)} fusion(bf16[512,256]{1,0:T(8,128)(2,1)S(1)} %bitcast.42, s32[1024]{0:T(1024)S(1)} %broadcast_clamp_fusion), kind=kCustom, calls=%fused_computation | custom fusion | bytes 1052672 | tf_op jit(solution)/shard_map/jit(_take)/gather | solution.py:173
  144.6 1.4 select_select_fusion
  146.2 8.6 %fusion.39 = f32[1024,5120]{1,0:T(8,128)} fusion(bf16[1024,256]{1,0:T(8,128)(2,1)S(1)} %select_select_fusion, bf16[5120,256]{1,0:T(8,128)(2,1)S(1)} %copy-done), kind=kOutput, calls=%fused_computation.73 | convolution fusion | flops 2684354560 | bytes 24117248 | tf_op jit(solution)/shard_map/dot_general | solution.py:175
  155.0 13.4 %multiply_add_fusion = f32[1024,5120]{1,0:T(8,128)} fusion(f32[1024,5120]{1,0:T(8,128)} %fusion.39, f32[1024,16]{0,1:T(8,128)S(1)} %fusion.40, bf16[5120,16]{0,1:T(8,128)(2,1)S(1)} %copy-done.7), kind=kOutput, calls=%fused_computation.2 | convolution fusion | flops 178257920 | bytes 42172416 | tf_op jit(solution)/shard_map/dot_general | solution.py:187
  168.4 15.5 %pad_maximum_fusion = f32[1024,5136]{1,0:T(8,128)} fusion(f32[1024,16]{1,0:T(8,128)S(1)} %copy.37, f32[1024,5120]{1,0:T(8,128)} %multiply_add_fusion), kind=kLoop, calls=%fused_computation.1 | loop fusion | flops 5259264 | bytes 42074112 | tf_op jit(solution)/shard_map/concatenate | solution.py:28
  184.0 4.3 convolution_multiply_fusion.1
  188.3 5.0 %convolution_multiply_fusion.3 = f32[16,1024]{1,0:T(8,128)} fusion(bf16[256,1024]{1,0:T(8,128)(2,1)} %param.16, bf16[8192,16]{0,1:T(8,128)(2,1)} %param.19, bf16[256,8192]{1,0:T(8,128)(2,1)} %param.14, f32[8192]{0:T(1024)S(1)} %copy-done.8, f32[256]{0:T(256)S(1)} %get-tuple-element.13), kind=kOutput, calls=%fused_computation.28 | convolution fusion | flops 83906560 | bytes 5080064 | tf_op jit(solution)/shard_map/dot_general | solution.py:106
  193.3 117.6 %reduce-scatter.2.cloned.1.call-done = f32[32,5136]{1,0:T(8,128)} async-done(((f32[1024,5136]{1,0:T(8,128)}), f32[32,5136]{1,0:T(8,128)}) %reduce-scatter.2.cloned.1.call-update) | async-done | bytes 657424 | tf_op jit(solution)/shard_map/reduce_scatter | solution.py:29
  310.8 2.1 fusion.24
  312.9 1.1 convolution_convert_fusion.2
  314.1 1.7 convolution_multiply_fusion.2
  315.9 13.6 %all_to_all.42 = bf16[32,2,256]{2,1,0:T(2,128)(2,1)S(1)} all-to-all(bf16[32,2,256]{2,1,0:T(2,128)(2,1)S(1)} %reshape.107), channel_id=1, replica_groups=mesh['dp'=4,'fsdp'=8,'enc'=4] {'fsdp','enc'}, dimensions={0} | all-to-all | bytes 65536 | tf_op jit(solution)/shard_map/all_to_all | solution.py:19
  330.1 8.2 %all_to_all.43 = f32[4,16,256]{2,1,0:T(8,128)S(1)} all-to-all(f32[4,16,256]{2,1,0:T(8,128)S(1)} %broadcast_in_dim.81), channel_id=1, replica_groups=mesh['dp'=4,'fsdp'=8,'enc'=4] {'dp'}, dimensions={0} | all-to-all | bytes 131072 | tf_op jit(solution)/shard_map/all_to_all | solution.py:19
  338.3 0.6 reduce_sum.52
  338.9 126.5 %all-reduce.4.cloned.1.call-done = (f32[8192,16]{0,1:T(8,128)}, f32[16,1024]{1,0:T(8,128)}, f32[5120,16]{0,1:T(8,128)}) async-done(((f32[8192,16]{0,1:T(8,128)}, f32[16,1024]{1,0:T(8,128)}, f32[5120,16]{0,1:T(8,128)}), (f32[8192,16]{0,1:T(8,128)}, f32[16,1024]{1,0:T(8,128)}, f32[5120,16]{0,1:T(8,128)})) %all-reduce.4.cloned.1.call-update) | async-done | bytes 917520 | tf_op jit(solution)/shard_map/psum | solution.py:204
  465.4 1.9 copy.47
  467.3 1.5 copy.48
  468.8 1.7 copy.49
  (52 shorter events, 2.9 us)
Async XLA Ops:
  7.2 139.1 %copy-start = (bf16[5120,256]{1,0:T(8,128)(2,1)S(1)}, bf16[5120,256]{1,0:T(8,128)(2,1)}, u32[]{:S(2)}) copy-start(bf16[5120,256]{1,0:T(8,128)(2,1)} %param.21) | copy-start | bytes 7864324
  7.2 38.2 %all-gather.2.cloned.1.call-start = ((), (), s32[]{:S(2)}) async-start(), calls=%async_computation.5 | async-start | bytes 4718592 | tf_op jit(solution)/shard_map/all_gather | solution.py:147
  54.8 5.5 %copy-start.12 = (s32[32]{0:T(128)S(1)}, s32[32]{0:T(128)}, u32[]{:S(2)}) copy-start(s32[32]{0:T(128)} %param.25) | copy-start | bytes 388
  54.8 6.1 %copy-start.11 = (s32[32]{0:T(128)S(1)}, s32[32]{0:T(128)}, u32[]{:S(2)}) copy-start(s32[32]{0:T(128)} %param.26) | copy-start | bytes 388
  54.9 7.1 %copy-start.6 = (bf16[256,1024]{1,0:T(8,128)(2,1)S(1)}, bf16[256,1024]{1,0:T(8,128)(2,1)}, u32[]{:S(2)}) copy-start(bf16[256,1024]{1,0:T(8,128)(2,1)} %param.16) | copy-start | bytes 1572868
  54.9 7.2 %copy-start.9 = (bf16[16,1024]{1,0:T(8,128)(2,1)S(1)}, bf16[16,1024]{1,0:T(8,128)(2,1)}, u32[]{:S(2)}) copy-start(bf16[16,1024]{1,0:T(8,128)(2,1)} %param.20) | copy-start | bytes 98308
  54.9 53.7 %all-to-all-start = ((bf16[8,256,1024]{2,1,0:T(8,128)(2,1)}), bf16[8,256,1024]{2,1,0:T(8,128)(2,1)}, u32[]{:S(2)}, u32[]{:S(2)}) async-start(bf16[8,256,1024]{2,1,0:T(8,128)(2,1)} %bitcast.44), calls=%async_computation | async-start | bytes 8388608 | tf_op jit(solution)/shard_map/all_to_all | solution.py:152
  111.7 1.7 copy-start.8
  113.4 5.0 %copy-start.2 = (bf16[256,8192]{1,0:T(8,128)(2,1)S(1)}, bf16[256,8192]{1,0:T(8,128)(2,1)}, u32[]{:S(2)}) copy-start(bf16[256,8192]{1,0:T(8,128)(2,1)} %param.14) | copy-start | bytes 12582916
  113.4 5.0 %copy-start.4 = (bf16[256,8192]{1,0:T(8,128)(2,1)S(1)}, bf16[256,8192]{1,0:T(8,128)(2,1)}, u32[]{:S(2)}) copy-start(bf16[256,8192]{1,0:T(8,128)(2,1)} %param.15) | copy-start | bytes 12582916
  121.8 2.0 copy-start.3
  123.8 22.1 %copy-start.10 = (bf16[16,256]{1,0:T(8,128)(2,1)S(1)}, bf16[16,256]{1,0:T(8,128)(2,1)}, u32[]{:S(2)}) copy-start(bf16[16,256]{1,0:T(8,128)(2,1)} %param.23) | copy-start | bytes 24580
  124.7 14.9 %all-to-all-start.1 = ((bf16[16,32,256]{2,0,1:T(8,128)(2,1)}), bf16[16,32,256]{2,0,1:T(8,128)(2,1)S(1)}, u32[]{:S(2)}, u32[]{:S(2)}) async-start(bf16[16,32,256]{2,0,1:T(8,128)(2,1)} %bitcast.38), calls=%async_computation.1 | async-start | bytes 524288 | tf_op jit(solution)/shard_map/all_to_all | solution.py:168
  130.8 180.0 %reduce-scatter.2.cloned.1.call-start = ((), (), s32[]{:S(2)}) async-start(), calls=%async_computation.6 | async-start | bytes 22167552 | tf_op jit(solution)/shard_map/reduce_scatter | solution.py:29
  146.2 8.8 %copy-start.7 = (bf16[5120,16]{0,1:T(8,128)(2,1)S(1)}, bf16[5120,16]{0,1:T(8,128)(2,1)}, u32[]{:S(2)}) copy-start(bf16[5120,16]{0,1:T(8,128)(2,1)} %param.22) | copy-start | bytes 491524
  183.9 126.9 %copy-start.5 = (bf16[32,5120]{1,0:T(8,128)(2,1)S(1)}, bf16[32,5120]{1,0:T(8,128)(2,1)}, u32[]{:S(2)}) copy-start(bf16[32,5120]{1,0:T(8,128)(2,1)} %param.24) | copy-start | bytes 983044
  183.9 281.5 %all-reduce.4.cloned.1.call-start = ((), (), s32[]{:S(2)}) async-start(), calls=%async_computation.7 | async-start | bytes 1835008 | tf_op jit(solution)/shard_map/psum | solution.py:204
  184.0 286.5 %copy-start.1 = (bf16[5120,256]{1,0:T(8,128)(2,1)S(1)}, bf16[5120,256]{1,0:T(8,128)(2,1)}, u32[]{:S(2)}) copy-start(bf16[5120,256]{1,0:T(8,128)(2,1)} %param.21) | copy-start | bytes 7864324
Sparse Core Ops, SparseCore 0:
  9.7 35.6 all-gather.1
  184.0 126.7 reduce-scatter.1
  316.7 148.6 all-reduce.3
where the time goes:
time: 478 us; the launch traced here: 477 us
  waiting for transfers between devices  337 us (71%)
  matrix products  49.1 us (10%)
  other arithmetic  27.4 us (6%)
  blocking collectives  21.8 us (5%)
  local copies, waits for them, and re-layouts  15.8 us (3%)
  between operations  14.7 us (3%)
  starting transfers between devices  11.3 us (2%)
    psum x1, waiting for transfers between devices, body(): lax.psum((scale_factor * down_term, scale_factor * up_term, scale_factor...  127 us
    reduce_scatter x1, waiting for transfers between devices, in_one_piece(): out = lax.psum_scatter(both, axis, scatter_dimension=dim, tiled=True)  118 us
    all_to_all x1, waiting for transfers between devices, body(): lax.all_to_all(columns, 'fsdp', split_axis=0, concat_axis=1, tiled=True)  46.3 us
    all_gather x1, waiting for transfers between devices, body(): lax.all_gather(value_output_gradient, 'fsdp', axis=0, tiled=True)  37.5 us
    all_to_all x2, blocking collectives, sent_to_all(): return lax.all_to_all(copies, axis, split_axis=0, concat_axis=0, tiled=True)  21.8 us
    concatenate x1, other arithmetic, in_one_piece(): both = jnp.concatenate(arrays, axis=along)  15.5 us
    dot_general x1, matrix products, body(): jnp.dot(low_part, merger_down_factor.astype(jnp.float32).T)  13.4 us
  transfers between devices with their start and end apart: 5, of which 5 were waited for; matrix products, arithmetic and copies ran while one was open for 3% of the time, Pallas kernels for 0%

commit v1 on v0

--- a/solution.py
+++ b/solution.py
@@ -144,7 +144,12 @@
     )
     all_low = gathered_copies(act_low, ("fsdp", "enc"), 0)
     columns = lax.dot_general(
-        lax.all_gather(value_output_gradient, "fsdp", axis=0, tiled=True),
+        jnp.concatenate(
+            lax.all_to_all(
+                jnp.stack([value_output_gradient] * lax.axis_size("fsdp")), "fsdp", 0, 0
+            ),
+            axis=0,
+        ),
         value_frozen_weight,
         (((1,), (1,)), ((), ())),
         preferred_element_type=jnp.float32,

time: 478 us -> 495 us (1.036)
  blocking collectives: 21.8 us -> 76.3 us
  waiting for transfers between devices: 337 us -> 299 us
    all_to_all x0 -> x1, blocking collectives: none -> 54.4 us  [body(): lax.all_to_all(jnp.stack([value_output_gradient] * lax.axis_size('fsdp'))...]
    all_gather x1 -> x0, waiting for transfers between devices: 37.5 us -> none  [body(): lax.all_gather(value_output_gradient, 'fsdp', axis=0, tiled=True)]
  transfers between devices with their start and end apart: 5 -> 4, of which waited for: 5 -> 4; matrix products, arithmetic and copies ran while one was open for 3% -> 3% of each run, Pallas kernels for 0% -> 0%
where the time goes in v1:
time: 495 us; the launch traced here: 494 us
  waiting for transfers between devices  299 us (60%)
  blocking collectives  76.3 us (15%)
  matrix products  46.2 us (9%)
  other arithmetic  27.4 us (6%)
  local copies, waits for them, and re-layouts  17.5 us (4%)
  between operations  15 us (3%)
  starting transfers between devices  12.9 us (3%)
    psum x1, waiting for transfers between devices, body(): lax.psum((scale_factor * down_term, scale_factor * up_term, scale_factor...  126 us
    reduce_scatter x1, waiting for transfers between devices, in_one_piece(): out = lax.psum_scatter(both, axis, scatter_dimension=dim, tiled=True)  118 us
    all_to_all x1, blocking collectives, body(): lax.all_to_all(jnp.stack([value_output_gradient] * lax.axis_size('fsdp'))...  54.4 us
    all_to_all x1, waiting for transfers between devices, body(): lax.all_to_all(columns, 'fsdp', split_axis=0, concat_axis=1, tiled=True)  46.3 us
    all_to_all x2, blocking collectives, sent_to_all(): return lax.all_to_all(copies, axis, split_axis=0, concat_axis=0, tiled=True)  21.9 us
    concatenate x1, other arithmetic, in_one_piece(): both = jnp.concatenate(arrays, axis=along)  15.5 us
    dot_general x1, matrix products, body(): jnp.dot(low_part, merger_down_factor.astype(jnp.float32).T)  13.6 us
  transfers between devices with their start and end apart: 4, of which 4 were waited for; matrix products, arithmetic and copies ran while one was open for 3% of the time, Pallas kernels for 0%

profile of v1, /device:TPU:1, one launch (start us, length us, event | category | flops | bytes accessed | tf_op | source)
XLA Modules:
  0.0 494.0 jit_solution(8538102132644149656)
XLA Ops:
  7.2 1.7 stack.2
  8.9 54.4 %all_to_all.47 = bf16[8,256,1024]{2,1,0:T(8,128)(2,1)S(1)} all-to-all(bf16[8,256,1024]{2,1,0:T(8,128)(2,1)S(1)} %stack.2), channel_id=1, replica_groups=mesh['dp'=4,'fsdp'=8,'enc'=4] {'fsdp'}, dimensions={0} | all-to-all | bytes 8388608 | tf_op jit(solution)/shard_map/all_to_all | solution.py:148
  63.3 6.2 %convolution_convert_fusion = bf16[2048,1024]{1,0:T(8,128)(2,1)} fusion(bf16[2048,1024]{1,0:T(8,128)(2,1)S(1)} %bitcast.46, bf16[1024,1024]{1,0:T(8,128)(2,1)S(1)} %copy-done.13), kind=kOutput, calls=%fused_computation.21 | convolution fusion | flops 4297064448 | bytes 10485760 | tf_op jit(solution)/shard_map/dot_general | solution.py:146
  69.6 5.6 %all-to-all-start.1 = ((bf16[8,256,1024]{2,1,0:T(8,128)(2,1)}), bf16[8,256,1024]{2,1,0:T(8,128)(2,1)}, u32[]{:S(2)}, u32[]{:S(2)}) async-start(bf16[8,256,1024]{2,1,0:T(8,128)(2,1)} %bitcast.45), calls=%async_computation.1 | async-start | bytes 8388608 | tf_op jit(solution)/shard_map/all_to_all | solution.py:157
  76.7 0.7 iota_compare_fusion.1
  77.7 46.3 %all-to-all-done.1 = bf16[8,256,1024]{2,1,0:T(8,128)(2,1)} async-done(((bf16[8,256,1024]{2,1,0:T(8,128)(2,1)}), bf16[8,256,1024]{2,1,0:T(8,128)(2,1)}, u32[]{:S(2)}, u32[]{:S(2)}) %all-to-all-start.1) | async-done | bytes 4194336 | tf_op jit(solution)/shard_map/all_to_all | solution.py:157
  124.0 3.2 convert_bitcast_fusion
  127.2 1.7 copy.40
  128.9 4.9 fusion.2
  133.9 3.4 fusion.5
  137.3 2.0 copy-done.3
  139.4 0.7 copy.42
  140.2 7.0 %all-to-all-start.2 = ((bf16[16,32,256]{2,0,1:T(8,128)(2,1)}), bf16[16,32,256]{2,0,1:T(8,128)(2,1)S(1)}, u32[]{:S(2)}, u32[]{:S(2)}) async-start(bf16[16,32,256]{2,0,1:T(8,128)(2,1)} %bitcast.39), calls=%async_computation.2 | async-start | bytes 524288 | tf_op jit(solution)/shard_map/all_to_all | solution.py:173
  147.6 8.4 %all-to-all-done.2 = bf16[16,32,256]{2,0,1:T(8,128)(2,1)S(1)} async-done(((bf16[16,32,256]{2,0,1:T(8,128)(2,1)}), bf16[16,32,256]{2,0,1:T(8,128)(2,1)S(1)}, u32[]{:S(2)}, u32[]{:S(2)}) %all-to-all-start.2) | async-done | bytes 262176 | tf_op jit(solution)/shard_map/all_to_all | solution.py:173
  156.0 5.0 %gather_fusion = bf16[1024,256]{1,0:T(8,128)(2,1)} fusion(bf16[512,256]{1,0:T(8,128)(2,1)S(1)} %bitcast.43, s32[1024]{0:T(1024)S(1)} %broadcast_clamp_fusion), kind=kCustom, calls=%fused_computation | custom fusion | bytes 1052672 | tf_op jit(solution)/shard_map/jit(_take)/gather | solution.py:178
  161.0 1.4 select_select_fusion
  162.6 8.7 %fusion.39 = f32[1024,5120]{1,0:T(8,128)} fusion(bf16[1024,256]{1,0:T(8,128)(2,1)S(1)} %select_select_fusion, bf16[5120,256]{1,0:T(8,128)(2,1)S(1)} %copy-done), kind=kOutput, calls=%fused_computation.73 | convolution fusion | flops 2684354560 | bytes 24117248 | tf_op jit(solution)/shard_map/dot_general | solution.py:180
  171.5 13.6 %multiply_add_fusion = f32[1024,5120]{1,0:T(8,128)} fusion(f32[1024,5120]{1,0:T(8,128)} %fusion.39, f32[1024,16]{0,1:T(8,128)S(1)} %fusion.40, bf16[5120,16]{0,1:T(8,128)(2,1)S(1)} %copy-done.7), kind=kOutput, calls=%fused_computation.2 | convolution fusion | flops 178257920 | bytes 42172416 | tf_op jit(solution)/shard_map/dot_general | solution.py:192
  185.1 15.5 %pad_maximum_fusion = f32[1024,5136]{1,0:T(8,128)} fusion(f32[1024,16]{1,0:T(8,128)S(1)} %copy.37, f32[1024,5120]{1,0:T(8,128)} %multiply_add_fusion), kind=kLoop, calls=%fused_computation.1 | loop fusion | flops 5259264 | bytes 42074112 | tf_op jit(solution)/shard_map/concatenate | solution.py:28
  200.7 4.3 convolution_multiply_fusion.1
  204.9 5.0 %convolution_multiply_fusion.3 = f32[16,1024]{1,0:T(8,128)} fusion(bf16[256,1024]{1,0:T(8,128)(2,1)} %param.16, bf16[8192,16]{0,1:T(8,128)(2,1)} %param.19, bf16[256,8192]{1,0:T(8,128)(2,1)} %param.14, f32[8192]{0:T(1024)S(1)} %copy-done.8, f32[256]{0:T(256)S(1)} %get-tuple-element.13), kind=kOutput, calls=%fused_computation.28 | convolution fusion | flops 83906560 | bytes 5080064 | tf_op jit(solution)/shard_map/dot_general | solution.py:106
  210.0 117.5 %reduce-scatter.2.cloned.1.call-done = f32[32,5136]{1,0:T(8,128)} async-done(((f32[1024,5136]{1,0:T(8,128)}), f32[32,5136]{1,0:T(8,128)}) %reduce-scatter.2.cloned.1.call-update) | async-done | bytes 657424 | tf_op jit(solution)/shard_map/reduce_scatter | solution.py:29
  327.5 2.1 fusion.24
  329.6 1.1 convolution_convert_fusion.2
  330.7 1.7 convolution_multiply_fusion.2
  332.6 13.6 %all_to_all.48 = bf16[32,2,256]{2,1,0:T(2,128)(2,1)S(1)} all-to-all(bf16[32,2,256]{2,1,0:T(2,128)(2,1)S(1)} %reshape.113), channel_id=1, replica_groups=mesh['dp'=4,'fsdp'=8,'enc'=4] {'fsdp','enc'}, dimensions={0} | all-to-all | bytes 65536 | tf_op jit(solution)/shard_map/all_to_all | solution.py:19
  346.7 8.2 %all_to_all.49 = f32[4,16,256]{2,1,0:T(8,128)S(1)} all-to-all(f32[4,16,256]{2,1,0:T(8,128)S(1)} %broadcast_in_dim.81), channel_id=1, replica_groups=mesh['dp'=4,'fsdp'=8,'enc'=4] {'dp'}, dimensions={0} | all-to-all | bytes 131072 | tf_op jit(solution)/shard_map/all_to_all | solution.py:19
  355.0 0.6 reduce_sum.52
  355.6 126.5 %all-reduce.4.cloned.1.call-done = (f32[8192,16]{0,1:T(8,128)}, f32[16,1024]{1,0:T(8,128)}, f32[5120,16]{0,1:T(8,128)}) async-done(((f32[8192,16]{0,1:T(8,128)}, f32[16,1024]{1,0:T(8,128)}, f32[5120,16]{0,1:T(8,128)}), (f32[8192,16]{0,1:T(8,128)}, f32[16,1024]{1,0:T(8,128)}, f32[5120,16]{0,1:T(8,128)})) %all-reduce.4.cloned.1.call-update) | async-done | bytes 917520 | tf_op jit(solution)/shard_map/psum | solution.py:209
  482.1 1.9 copy.47
  483.9 1.5 copy.48
  485.4 1.7 copy.49
  (53 shorter events, 2.9 us)
Async XLA Ops:
  7.2 155.4 %copy-start = (bf16[5120,256]{1,0:T(8,128)(2,1)S(1)}, bf16[5120,256]{1,0:T(8,128)(2,1)}, u32[]{:S(2)}) copy-start(bf16[5120,256]{1,0:T(8,128)(2,1)} %param.21) | copy-start | bytes 7864324
  7.2 56.1 %copy-start.13 = (bf16[1024,1024]{1,0:T(8,128)(2,1)S(1)}, bf16[1024,1024]{1,0:T(8,128)(2,1)}, u32[]{:S(2)}) copy-start(bf16[1024,1024]{1,0:T(8,128)(2,1)} %param.18) | copy-start | bytes 6291460
  69.6 6.3 %copy-start.12 = (s32[32]{0:T(128)S(1)}, s32[32]{0:T(128)}, u32[]{:S(2)}) copy-start(s32[32]{0:T(128)} %param.25) | copy-start | bytes 388
  69.6 6.9 %copy-start.11 = (s32[32]{0:T(128)S(1)}, s32[32]{0:T(128)}, u32[]{:S(2)}) copy-start(s32[32]{0:T(128)} %param.26) | copy-start | bytes 388
  69.6 7.9 %copy-start.6 = (bf16[256,1024]{1,0:T(8,128)(2,1)S(1)}, bf16[256,1024]{1,0:T(8,128)(2,1)}, u32[]{:S(2)}) copy-start(bf16[256,1024]{1,0:T(8,128)(2,1)} %param.16) | copy-start | bytes 1572868
  69.6 7.9 %copy-start.9 = (bf16[16,1024]{1,0:T(8,128)(2,1)S(1)}, bf16[16,1024]{1,0:T(8,128)(2,1)}, u32[]{:S(2)}) copy-start(bf16[16,1024]{1,0:T(8,128)(2,1)} %param.20) | copy-start | bytes 98308
  69.6 54.4 %all-to-all-start.1 = ((bf16[8,256,1024]{2,1,0:T(8,128)(2,1)}), bf16[8,256,1024]{2,1,0:T(8,128)(2,1)}, u32[]{:S(2)}, u32[]{:S(2)}) async-start(bf16[8,256,1024]{2,1,0:T(8,128)(2,1)} %bitcast.45), calls=%async_computation.1 | async-start | bytes 8388608 | tf_op jit(solution)/shard_map/all_to_all | solution.py:157
  127.2 1.7 copy-start.8
  128.9 5.0 %copy-start.2 = (bf16[256,8192]{1,0:T(8,128)(2,1)S(1)}, bf16[256,8192]{1,0:T(8,128)(2,1)}, u32[]{:S(2)}) copy-start(bf16[256,8192]{1,0:T(8,128)(2,1)} %param.14) | copy-start | bytes 12582916
  128.9 5.0 %copy-start.4 = (bf16[256,8192]{1,0:T(8,128)(2,1)S(1)}, bf16[256,8192]{1,0:T(8,128)(2,1)}, u32[]{:S(2)}) copy-start(bf16[256,8192]{1,0:T(8,128)(2,1)} %param.15) | copy-start | bytes 12582916
  137.3 2.0 copy-start.3
  139.3 23.0 %copy-start.10 = (bf16[16,256]{1,0:T(8,128)(2,1)S(1)}, bf16[16,256]{1,0:T(8,128)(2,1)}, u32[]{:S(2)}) copy-start(bf16[16,256]{1,0:T(8,128)(2,1)} %param.23) | copy-start | bytes 24580
  140.2 15.8 %all-to-all-start.2 = ((bf16[16,32,256]{2,0,1:T(8,128)(2,1)}), bf16[16,32,256]{2,0,1:T(8,128)(2,1)S(1)}, u32[]{:S(2)}, u32[]{:S(2)}) async-start(bf16[16,32,256]{2,0,1:T(8,128)(2,1)} %bitcast.39), calls=%async_computation.2 | async-start | bytes 524288 | tf_op jit(solution)/shard_map/all_to_all | solution.py:173
  147.2 180.3 %reduce-scatter.2.cloned.1.call-start = ((), (), s32[]{:S(2)}) async-start(), calls=%async_computation.6 | async-start | bytes 22167552 | tf_op jit(solution)/shard_map/reduce_scatter | solution.py:29
  162.6 8.9 %copy-start.7 = (bf16[5120,16]{0,1:T(8,128)(2,1)S(1)}, bf16[5120,16]{0,1:T(8,128)(2,1)}, u32[]{:S(2)}) copy-start(bf16[5120,16]{0,1:T(8,128)(2,1)} %param.22) | copy-start | bytes 491524
  200.6 126.9 %copy-start.5 = (bf16[32,5120]{1,0:T(8,128)(2,1)S(1)}, bf16[32,5120]{1,0:T(8,128)(2,1)}, u32[]{:S(2)}) copy-start(bf16[32,5120]{1,0:T(8,128)(2,1)} %param.24) | copy-start | bytes 983044
  200.6 281.5 %all-reduce.4.cloned.1.call-start = ((), (), s32[]{:S(2)}) async-start(), calls=%async_computation.7 | async-start | bytes 1835008 | tf_op jit(solution)/shard_map/psum | solution.py:209
  200.7 286.5 %copy-start.1 = (bf16[5120,256]{1,0:T(8,128)(2,1)S(1)}, bf16[5120,256]{1,0:T(8,128)(2,1)}, u32[]{:S(2)}) copy-start(bf16[5120,256]{1,0:T(8,128)(2,1)} %param.21) | copy-start | bytes 7864324
Sparse Core Ops, SparseCore 0:
  200.7 126.7 reduce-scatter.1
  333.3 148.7 all-reduce.3
